TPU v7x, 32 devices: a whole 2x2x4 slice. The times are simulated.
32 devices in a mesh: row: 4 (over z), col: 8 (over y, x, core).
Axes of the slice: x: 2, y: 2, z: 4, core: 2. Of those that a mesh axis runs over, the one named last changes fastest.
Arguments:
- node_feats: bfloat16 [4096, 512], P(('row', 'col')), may hold values from -80 to 80
- block_mask: int32 [32, 32], replicated, may hold values from 0 to 1, as said below
- w_qkv: bfloat16 [2, 512, 1536], replicated, may hold values from -0.25 to 0.25
- w_out: bfloat16 [2, 512, 512], replicated, may hold values from -0.79296875 to 0.79296875
- w_up: bfloat16 [2, 512, 1024], replicated, may hold values from -0.25 to 0.25
- w_down: bfloat16 [2, 1024, 512], replicated, may hold values from -0.1875 to 0.1875
- ln_gain: float32 [2, 2, 512], replicated, may hold values from 0.1 to 1.9
- ln_bias: float32 [2, 2, 512], replicated, may hold values from -3 to 3
Outputs:
- nodes_out: bfloat16 [4096, 512], P(('row', 'col'))
Inputs may be any that keep to these rules, and one draw needn't show every extreme that they name: `block_mask`: A symmetric 0/1 table over the 32 node blocks; every block is linked with itself.
All inputs are finite; a program needn't handle non-finite values.
Results may differ from a plain program's by a relative error of at most 0.022.
Values may be sent and summed in bfloat16 or wider, within the bound.
A program may use at most 128 MiB of HBM per device.

v0:
```python
import jax
import jax.numpy as jnp
from jax import lax
from jax.sharding import PartitionSpec as P

HEADS = 8
BLOCK = 128
LAYERS = 2


def combined_all(x, axis, combine):
    everything = jax.tree.map(
        lambda part, kind: lax.all_gather(part.astype(kind), axis),
        x,
        (jnp.bfloat16, jnp.bfloat16, jnp.bfloat16),
    )

    def take(k):
        return jax.tree.map(lambda part, own: part[k].astype(own.dtype), everything, x)

    return lax.fori_loop(
        1, lax.axis_size(axis), lambda k, so_far: combine(so_far, take(k)), take(0)
    )


def layer_norm(values, gain, bias):
    center = values - jnp.mean(values, axis=-1, keepdims=True)
    spread = jnp.mean(center * center, axis=-1, keepdims=True)
    return center * lax.rsqrt(spread + 1e-05) * gain + bias


def per_head(summed, factor):
    count = summed.shape[0]
    return (summed.reshape(count, factor.shape[1], -1) * factor[:, :, None]).reshape(summed.shape)


def combine(first, second):
    sum_a, peak_a, mass_a = first
    sum_b, peak_b, mass_b = second
    peak = jnp.maximum(peak_a, peak_b)
    scale_a = jnp.exp(peak_a - peak)
    scale_b = jnp.exp(peak_b - peak)
    return (
        per_head(sum_a, scale_a) + per_head(sum_b, scale_b),
        peak,
        mass_a * scale_a + mass_b * scale_b,
    )


def partial_attention(queries, keys, values, sub_mask, heads):
    qrows, width = queries.shape
    head_dim = width // heads
    qblock = min(512, qrows)
    nblocks = qrows // qblock
    qsplit = queries.reshape(nblocks, qblock, heads, head_dim)
    ksplit = keys.reshape(-1, heads, head_dim)
    vsplit = values.reshape(-1, heads, head_dim)
    mask_rows = sub_mask.reshape(nblocks, qblock // BLOCK, -1)

    def one_block(item):
        qpart, mpart = item
        scores = jnp.einsum("qhd,khd->hqk", qpart, ksplit, preferred_element_type=jnp.float32) * (
            1.0 / head_dim**0.5
        )
        allowed = (jnp.repeat(jnp.repeat(mpart, BLOCK, axis=0), BLOCK, axis=1) > 0)[None]
        peak = jnp.max(jnp.where(allowed, scores, -1e30), axis=-1, keepdims=True)
        weights = jnp.where(allowed, jnp.exp(scores - peak), 0.0)
        mass = jnp.sum(weights, axis=-1)
        summed = jnp.einsum(
            "hqk,khd->qhd", weights.astype(jnp.bfloat16), vsplit, preferred_element_type=jnp.float32
        )
        return (summed.reshape(qblock, width), peak[:, :, 0].T, mass.T)

    summed, peak, mass = lax.map(one_block, (qsplit, mask_rows))
    return (summed.reshape(qrows, width), peak.reshape(qrows, heads), mass.reshape(qrows, heads))


def per_device(node_feats, block_mask, w_qkv, w_out, w_up, w_down, ln_gain, ln_bias):
    rows, width = node_feats.shape
    heads = HEADS
    n_col = lax.axis_size("col")
    n_row = lax.axis_size("row")
    row_index = lax.axis_index("row")
    col_index = lax.axis_index("col")
    blk_dev = rows // BLOCK
    group_ids = row_index * (n_col * blk_dev) + jnp.arange(n_col * blk_dev, dtype=jnp.int32)
    column_ids = (
        (jnp.arange(n_row, dtype=jnp.int32)[:, None] * n_col + col_index) * blk_dev
        + jnp.arange(blk_dev, dtype=jnp.int32)[None, :]
    ).reshape(-1)
    query_ids, key_ids, own_start = (column_ids, group_ids, row_index * rows)
    sub_mask = jnp.take(jnp.take(block_mask, query_ids, axis=0), key_ids, axis=1)
    x = node_feats
    for layer in range(LAYERS):
        weights = w_qkv[layer]
        qkv = jnp.dot(x, weights, preferred_element_type=jnp.float32).astype(jnp.bfloat16)
        own_q = qkv[:, :width]
        pair = (qkv[:, width : 2 * width], qkv[:, 2 * width :])
        keys, values = (
            lax.all_gather(pair[0], "col", axis=0, tiled=True),
            lax.all_gather(pair[1], "col", axis=0, tiled=True),
        )
        queries = lax.all_gather(own_q, "row", axis=0, tiled=True)
        summed, peak, mass = partial_attention(queries, keys, values, sub_mask, heads)
        summed, peak, mass = combined_all((summed, peak, mass), "row", combine)
        summed = lax.dynamic_slice_in_dim(summed, own_start, rows, 0)
        mass = lax.dynamic_slice_in_dim(mass, own_start, rows, 0)
        attn = per_head(summed, 1.0 / mass).astype(jnp.bfloat16)
        mixed = jnp.dot(attn, w_out[layer], preferred_element_type=jnp.float32)
        hidden = layer_norm(
            x.astype(jnp.float32) + mixed, ln_gain[layer, 0], ln_bias[layer, 0]
        ).astype(jnp.bfloat16)
        up = jax.nn.gelu(jnp.dot(hidden, w_up[layer], preferred_element_type=jnp.float32)).astype(
            jnp.bfloat16
        )
        down = jnp.dot(up, w_down[layer], preferred_element_type=jnp.float32)
        x = layer_norm(
            hidden.astype(jnp.float32) + down, ln_gain[layer, 1], ln_bias[layer, 1]
        ).astype(jnp.bfloat16)
    return x


def solution(mesh):
    placed = (P(("row", "col"), None), P(), P(), P(), P(), P(), P(), P())
    return jax.shard_map(
        per_device, mesh=mesh, in_specs=placed, out_specs=P(("row", "col"), None), check_vma=False
    )
```

profile of v0, /device:TPU:0, one launch (start us, length us, event | category | flops | bytes accessed | tf_op | source)
XLA Modules:
  0.0 255.1 jit_solution(7514067950112595281)
XLA Ops:
  6.5 1.9 convolution_convert_fusion.1
  11.5 1.6 broadcast_in_dim.118
  13.4 17.4 %all_gather.43 = bf16[512,512]{1,0:T(8,128)(2,1)S(1)} all-gather(bf16[128,512]{1,0:T(8,128)(2,1)S(1)} %get-tuple-element.465), channel_id=1, replica_groups=mesh['row'=4,'col'=8] {'row'}, dimensions={0}, use_global_device_ids=true | all-gather | bytes 655360 | tf_op jit(solution)/shard_map/all_gather | solution.py:103
  31.0 4.4 %all-gather.13.cloned.1.call-done = bf16[1024,512]{1,0:T(8,128)(2,1)} async-done(((bf16[128,512]{1,0:T(8,128)(2,1)}), bf16[1024,512]{1,0:T(8,128)(2,1)}) %all-gather.13.cloned.1.call-update) | async-done | bytes 1048592 | tf_op jit(solution)/shard_map/all_gather | solution.py:100
  35.4 1.5 copy.33
  36.9 7.4 %select_reduce_fusion.1 = (f32[8,512]{1,0:T(8,128)S(1)}, f32[8,512,1024]{2,1,0:T(8,128)}) fusion(pred[512,1024]{1,0:T(8,128)(4,1)S(1)} %bitcast.172, bf16[512,8,64]{0,2,1:T(8,128)(2,1)S(1)} %bitcast.180, bf16[1024,8,64]{0,2,1:T(8,128)(2,1)S(1)} %bitcast.178), kind=kOutput, calls=%fused_computation.25 | convolution fusion | flops 549449728 | bytes 18890752 | tf_op jit(solution)/shard_map/while/body/eval_jaxpr/qhd,khd->hqk/dot_general | solution.py:62
  44.3 16.4 %all-gather.11.cloned.1.call-done = bf16[1024,512]{1,0:T(8,128)(2,1)} async-done(((bf16[128,512]{1,0:T(8,128)(2,1)}), bf16[1024,512]{1,0:T(8,128)(2,1)}) %all-gather.11.cloned.1.call-update) | async-done | bytes 1048592 | tf_op jit(solution)/shard_map/all_gather | solution.py:101
  60.7 1.5 copy.29
  62.2 7.6 %fusion.20 = bf16[8,64,512]{2,1,0:T(8,128)(2,1)S(1)} fusion(bf16[1024,8,64]{0,2,1:T(8,128)(2,1)S(1)} %bitcast.183, f32[8,512,1024]{2,1,0:T(8,128)} %get-tuple-element.476, f32[8,512]{1,0:T(8,128)S(1)} %get-tuple-element.475, pred[512,1024]{1,0:T(8,128)(4,1)S(1)} %bitcast.173), kind=kOutput, calls=%fused_computation.41 | convolution fusion | flops 553910272 | bytes 18890752 | tf_op jit(solution)/shard_map/while/body/eval_jaxpr/hqk,khd->qhd/dot_general | solution.py:69
  70.9 8.2 %fusion.6 = bf16[8,512]{1,0:T(8,128)(2,1)S(1)} fusion(f32[8,512,1024]{2,1,0:T(8,128)} %get-tuple-element.476, f32[8,512]{1,0:T(8,128)S(1)} %get-tuple-element.475, pred[512,1024]{1,0:T(8,128)(4,1)S(1)} %bitcast.174), kind=kLoop, calls=%fused_computation.26 | loop fusion | flops 16773120 | bytes 17326080 | tf_op jit(solution)/shard_map/while/body/eval_jaxpr/reduce_sum | solution.py:68
  79.2 13.9 %all-gather.1 = bf16[2048,8]{0,1:T(8,128)(2,1)S(1)} all-gather(bf16[512,8]{0,1:T(8,128)(2,1)S(1)} %bitcast.193), channel_id=3, replica_groups=mesh['row'=4,'col'=8] {'row'}, dimensions={0}, use_global_device_ids=true | all-gather | bytes 40960 | tf_op jit(solution)/shard_map/all_gather | solution.py:13
  93.1 13.7 %all-gather = bf16[2048,8]{0,1:T(8,128)(2,1)S(1)} all-gather(bf16[512,8]{0,1:T(8,128)(2,1)S(1)} %convert_bitcast_fusion.3), channel_id=2, replica_groups=mesh['row'=4,'col'=8] {'row'}, dimensions={0}, use_global_device_ids=true | all-gather | bytes 40960 | tf_op jit(solution)/shard_map/all_gather | solution.py:13
  106.8 10.9 %all-gather.15.cloned.1.call-done = bf16[4,512,512]{2,1,0:T(8,128)(2,1)} async-done(((bf16[1,512,512]{2,1,0:T(8,128)(2,1)}), bf16[4,512,512]{2,1,0:T(8,128)(2,1)}) %all-gather.15.cloned.1.call-update) | async-done | bytes 2097168 | tf_op jit(solution)/shard_map/all_gather | solution.py:13
  119.2 5.7 %while.24 = (s32[]{:T(128)}, f32[512,512]{0,1:T(8,128)S(1)}, f32[512,8]{0,1:T(8,128)S(1)}, f32[512,8]{0,1:T(8,128)S(1)}, bf16[4,512,8]{1,2,0:T(8,128)(2,1)S(1)},...) while((s32[]{:T(128)}, f32[512,512]{0,1:T(8,128)S(1)}, ...), condition=%wide.region_3.4_spmd, body=%wide.region_2.3_spmd.sunk | while | flops 1081349 | bytes 4866191 | solution.py:21
  125.0 1.4 fusion.117
  126.6 2.2 fusion.118
  129.0 1.8 convolution_convert_fusion
  132.3 15.7 %all_gather.49 = bf16[512,512]{1,0:T(8,128)(2,1)S(1)} all-gather(bf16[128,512]{1,0:T(8,128)(2,1)S(1)} %get-tuple-element.462), channel_id=1, replica_groups=mesh['row'=4,'col'=8] {'row'}, dimensions={0}, use_global_device_ids=true | all-gather | bytes 655360 | tf_op jit(solution)/shard_map/all_gather | solution.py:103
  148.2 5.7 %all-gather.19.cloned.1.call-done = bf16[1024,512]{1,0:T(8,128)(2,1)} async-done(((bf16[128,512]{1,0:T(8,128)(2,1)}), bf16[1024,512]{1,0:T(8,128)(2,1)}) %all-gather.19.cloned.1.call-update) | async-done | bytes 1048592 | tf_op jit(solution)/shard_map/all_gather | solution.py:100
  154.0 1.5 copy.39
  155.5 7.4 %select_reduce_fusion = (f32[8,512]{1,0:T(8,128)S(1)}, f32[8,512,1024]{2,1,0:T(8,128)}) fusion(pred[512,1024]{1,0:T(8,128)(4,1)S(1)} %bitcast.175, bf16[512,8,64]{0,2,1:T(8,128)(2,1)S(1)} %bitcast.181, bf16[1024,8,64]{0,2,1:T(8,128)(2,1)S(1)} %bitcast.179), kind=kOutput, calls=%fused_computation.23 | convolution fusion | flops 549449728 | bytes 18890752 | tf_op jit(solution)/shard_map/while/body/eval_jaxpr/qhd,khd->hqk/dot_general | solution.py:62
  162.9 16.2 %all-gather.17.cloned.1.call-done = bf16[1024,512]{1,0:T(8,128)(2,1)} async-done(((bf16[128,512]{1,0:T(8,128)(2,1)}), bf16[1024,512]{1,0:T(8,128)(2,1)}) %all-gather.17.cloned.1.call-update) | async-done | bytes 1048592 | tf_op jit(solution)/shard_map/all_gather | solution.py:101
  179.1 1.5 copy.37
  180.6 7.6 %fusion.23 = bf16[8,64,512]{2,1,0:T(8,128)(2,1)S(1)} fusion(bf16[1024,8,64]{0,2,1:T(8,128)(2,1)S(1)} %bitcast.184, f32[8,512,1024]{2,1,0:T(8,128)} %get-tuple-element.482, f32[8,512]{1,0:T(8,128)S(1)} %get-tuple-element.481, pred[512,1024]{1,0:T(8,128)(4,1)S(1)} %bitcast.176), kind=kOutput, calls=%fused_computation.42 | convolution fusion | flops 553910272 | bytes 18890752 | tf_op jit(solution)/shard_map/while/body/eval_jaxpr/hqk,khd->qhd/dot_general | solution.py:69
  189.2 8.2 %fusion.8 = bf16[8,512]{1,0:T(8,128)(2,1)S(1)} fusion(f32[8,512,1024]{2,1,0:T(8,128)} %get-tuple-element.482, f32[8,512]{1,0:T(8,128)S(1)} %get-tuple-element.481, pred[512,1024]{1,0:T(8,128)(4,1)S(1)} %bitcast.177), kind=kLoop, calls=%fused_computation.28 | loop fusion | flops 16773120 | bytes 17326080 | tf_op jit(solution)/shard_map/while/body/eval_jaxpr/reduce_sum | solution.py:68
  197.5 13.7 %all-gather.3 = bf16[2048,8]{0,1:T(8,128)(2,1)S(1)} all-gather(bf16[512,8]{0,1:T(8,128)(2,1)S(1)} %bitcast.192), channel_id=5, replica_groups=mesh['row'=4,'col'=8] {'row'}, dimensions={0}, use_global_device_ids=true | all-gather | bytes 40960 | tf_op jit(solution)/shard_map/all_gather | solution.py:13
  211.2 13.8 %all-gather.2 = bf16[2048,8]{0,1:T(8,128)(2,1)S(1)} all-gather(bf16[512,8]{0,1:T(8,128)(2,1)S(1)} %convert_bitcast_fusion.1), channel_id=4, replica_groups=mesh['row'=4,'col'=8] {'row'}, dimensions={0}, use_global_device_ids=true | all-gather | bytes 40960 | tf_op jit(solution)/shard_map/all_gather | solution.py:13
  225.0 11.1 %all-gather.21.cloned.1.call-done = bf16[4,512,512]{2,1,0:T(8,128)(2,1)} async-done(((bf16[1,512,512]{2,1,0:T(8,128)(2,1)}), bf16[4,512,512]{2,1,0:T(8,128)(2,1)}) %all-gather.21.cloned.1.call-update) | async-done | bytes 2097168 | tf_op jit(solution)/shard_map/all_gather | solution.py:13
  236.1 1.2 fusion.64
  237.6 5.7 %while.25 = (s32[]{:T(128)}, f32[512,512]{0,1:T(8,128)S(1)}, f32[512,8]{0,1:T(8,128)S(1)}, f32[512,8]{0,1:T(8,128)S(1)}, bf16[4,512,8]{1,2,0:T(8,128)(2,1)S(1)},...) while((s32[]{:T(128)}, f32[512,512]{0,1:T(8,128)S(1)}, ...), condition=%wide.region_11.12_spmd, body=%wide.region_10.11_spmd.sunk | while | flops 1081349 | bytes 4866191 | solution.py:21
  243.4 1.4 fusion.121
  245.0 2.2 fusion.122
  (94 shorter events, 21.9 us)
Async XLA Ops:
  6.5 3.5 %copy-start = (s32[32,32]{1,0:T(8,128)S(1)}, s32[32,32]{1,0:T(8,128)}, u32[]{:S(2)}) copy-start(s32[32,32]{1,0:T(8,128)} %param.13) | copy-start | bytes 12292
  6.5 28.9 %all-gather.13.cloned.1.call-start = ((), (), s32[]{:S(2)}) async-start(), calls=%async_computation.1 | async-start | bytes 1179648 | tf_op jit(solution)/shard_map/all_gather | solution.py:100
  9.2 51.5 %all-gather.11.cloned.1.call-start = ((), (), s32[]{:S(2)}) async-start(), calls=%async_computation | async-start | bytes 1179648 | tf_op jit(solution)/shard_map/all_gather | solution.py:101
  9.9 107.8 %all-gather.15.cloned.1.call-start = ((), (), s32[]{:S(2)}) async-start(), calls=%async_computation.2 | async-start | bytes 2621440 | tf_op jit(solution)/shard_map/all_gather | solution.py:13
  44.3 26.6 %copy-start.3 = (f32[2,2,512]{2,1,0:T(2,128)S(1)}, f32[2,2,512]{2,1,0:T(2,128)}, u32[]{:S(2)}) copy-start(f32[2,2,512]{2,1,0:T(2,128)} %param.18) | copy-start | bytes 24580
  44.3 26.6 %copy-start.4 = (f32[2,2,512]{2,1,0:T(2,128)S(1)}, f32[2,2,512]{2,1,0:T(2,128)}, u32[]{:S(2)}) copy-start(f32[2,2,512]{2,1,0:T(2,128)} %param.19) | copy-start | bytes 24580
  70.8 83.1 %all-gather.19.cloned.1.call-start = ((), (), s32[]{:S(2)}) async-start(), calls=%async_computation.4 | async-start | bytes 1179648 | tf_op jit(solution)/shard_map/all_gather | solution.py:100
  79.2 45.8 %copy-start.2 = (bf16[128,512]{1,0:T(8,128)(2,1)S(1)}, bf16[128,512]{1,0:T(8,128)(2,1)}, u32[]{:S(2)}) copy-start(bf16[128,512]{1,0:T(8,128)(2,1)} %param.12) | copy-start | bytes 393220
  131.6 47.5 %all-gather.17.cloned.1.call-start = ((), (), s32[]{:S(2)}) async-start(), calls=%async_computation.3 | async-start | bytes 1179648 | tf_op jit(solution)/shard_map/all_gather | solution.py:101
  132.2 103.9 %all-gather.21.cloned.1.call-start = ((), (), s32[]{:S(2)}) async-start(), calls=%async_computation.5 | async-start | bytes 2621440 | tf_op jit(solution)/shard_map/all_gather | solution.py:13
  236.1 12.1 %copy-start.1 = (s32[32,32]{1,0:T(8,128)S(1)}, s32[32,32]{1,0:T(8,128)}, u32[]{:S(2)}) copy-start(s32[32,32]{1,0:T(8,128)} %param.13) | copy-start | bytes 12292
Sparse Core Ops, SparseCore 0:
  9.3 26.0 all-gather.12
  37.3 23.3 all-gather.10
  71.0 46.6 all-gather.14
  131.8 22.1 all-gather.18
  155.7 23.3 all-gather.16
  189.4 46.6 all-gather.20
where the time goes:
time: 256 us; the launch traced here: 255 us
  blocking collectives  88.2 us (34%)
  waiting for transfers between devices  66.1 us (26%)
  matrix products  41 us (16%)
  other arithmetic  24.1 us (9%)
  local copies, waits for them, and re-layouts  21.5 us (8%)
  between operations  13.8 us (5%)
    all_gather x4, blocking collectives, combined_all(): lax.all_gather(part.astype(kind), axis)  55.1 us
    all_gather x2, blocking collectives, per_device(): queries = lax.all_gather(own_q, 'row', axis=0, tiled=True)  33.1 us
    all_gather x2, waiting for transfers between devices, per_device(): lax.all_gather(pair[1], 'col', axis=0, tiled=True)  32.6 us
    all_gather x2, waiting for transfers between devices, combined_all(): lax.all_gather(part.astype(kind), axis)  22 us
    reduce_sum x2, other arithmetic, one_block(): mass = jnp.sum(weights, axis=-1)  16.4 us
    dot_general x2, matrix products, one_block(): jnp.einsum('hqk,khd->qhd', weights.astype(jnp.bfloat16), vsplit, preferre...  15.2 us
    dot_general x2, matrix products, one_block(): jnp.einsum('qhd,khd->hqk', qpart, ksplit, preferred_element_type=jnp.floa...  14.8 us
    all_gather x2, waiting for transfers between devices, per_device(): lax.all_gather(pair[0], 'col', axis=0, tiled=True)  10.1 us
  transfers between devices with their start and end apart: 6, of which 6 were waited for; matrix products, arithmetic and copies ran while one was open for 15% of the time, Pallas kernels for 0%

commit v1 on v0

--- a/solution.py
+++ b/solution.py
@@ -6,6 +6,29 @@
 HEADS = 8
 BLOCK = 128
 LAYERS = 2
+
+
+def joined_along(tiles, dim):
+    shape = list(tiles.shape[1:])
+    shape[dim] *= tiles.shape[0]
+    return jnp.moveaxis(tiles, 0, dim).reshape(shape)
+
+
+def grow_blocks(x, axis):
+    count, place = (lax.axis_size(axis), lax.axis_index(axis))
+    blocks, bit = (x[None], 1)
+    while bit < count:
+        received = lax.ppermute(blocks, axis, [(i, i ^ bit) for i in range(count)])
+        low = place & bit == 0
+        blocks = jnp.concatenate(
+            [jnp.where(low, blocks, received), jnp.where(low, received, blocks)]
+        )
+        bit *= 2
+    return blocks
+
+
+def doubled_up(value, axis, dim):
+    return joined_along(grow_blocks(value, axis), dim)
 
 
 def combined_all(x, axis, combine):
@@ -97,7 +120,7 @@
         own_q = qkv[:, :width]
         pair = (qkv[:, width : 2 * width], qkv[:, 2 * width :])
         keys, values = (
-            lax.all_gather(pair[0], "col", axis=0, tiled=True),
+            doubled_up(pair[0], "col", 0),
             lax.all_gather(pair[1], "col", axis=0, tiled=True),
         )
         queries = lax.all_gather(own_q, "row", axis=0, tiled=True)

time: 256 us -> 233 us (0.910)
  waiting for transfers between devices: 66.1 us -> 34 us
  starting transfers between devices: 0.2 us -> 8.4 us
  other arithmetic: 24.1 us -> 27 us
    all_gather x2, waiting for transfers between devices: 32.6 us -> 0.01 us  [per_device(): lax.all_gather(pair[1], 'col', axis=0, tiled=True)]
    ppermute x0 -> x6, waiting for transfers between devices: none -> 14.4 us  [grow_blocks(): received = lax.ppermute(blocks, axis, [(i, i ^ bit) for i in range(count)])]
    all_gather x2 -> x0, waiting for transfers between devices: 10.1 us -> none  [per_device(): lax.all_gather(pair[0], 'col', axis=0, tiled=True)]
    ppermute x0 -> x6, starting transfers between devices: none -> 8.27 us  [grow_blocks(): received = lax.ppermute(blocks, axis, [(i, i ^ bit) for i in range(count)])]
    all_gather x2 -> x0, local copies, waits for them, and re-layouts: 2.96 us -> none  [per_device(): lax.all_gather(pair[0], 'col', axis=0, tiled=True)]
  transfers between devices with their start and end apart: 6 -> 10, of which waited for: 6 -> 6; matrix products, arithmetic and copies ran while one was open for 15% -> 17% of each run, Pallas kernels for 0% -> 0%
where the time goes in v1:
time: 233 us; the launch traced here: 232 us
  blocking collectives  87.3 us (37%)
  matrix products  40.9 us (18%)
  waiting for transfers between devices  34 us (15%)
  other arithmetic  27 us (12%)
  local copies, waits for them, and re-layouts  21 us (9%)
  between operations  13.6 us (6%)
  starting transfers between devices  8.4 us (4%)
    all_gather x4, blocking collectives, combined_all(): lax.all_gather(part.astype(kind), axis)  55.9 us
    all_gather x2, blocking collectives, per_device(): queries = lax.all_gather(own_q, 'row', axis=0, tiled=True)  31.3 us
    all_gather x2, waiting for transfers between devices, combined_all(): lax.all_gather(part.astype(kind), axis)  19.6 us
    reduce_sum x2, other arithmetic, one_block(): mass = jnp.sum(weights, axis=-1)  16.6 us
    dot_general x2, matrix products, one_block(): jnp.einsum('hqk,khd->qhd', weights.astype(jnp.bfloat16), vsplit, preferre...  15.2 us
    dot_general x2, matrix products, one_block(): jnp.einsum('qhd,khd->hqk', qpart, ksplit, preferred_element_type=jnp.floa...  14.7 us
    ppermute x6, waiting for transfers between devices, grow_blocks(): received = lax.ppermute(blocks, axis, [(i, i ^ bit) for i in range(count)])  14.4 us
    ppermute x6, starting transfers between devices, grow_blocks(): received = lax.ppermute(blocks, axis, [(i, i ^ bit) for i in range(count)])  8.27 us
  transfers between devices with their start and end apart: 10, of which 6 were waited for; matrix products, arithmetic and copies ran while one was open for 17% of the time, Pallas kernels for 0%

profile of v1, /device:TPU:0, one launch (start us, length us, event | category | flops | bytes accessed | tf_op | source)
XLA Modules:
  0.0 232.3 jit_solution(8189530725284435670)
XLA Ops:
  6.5 1.9 convolution_convert_fusion.1
  10.6 2.9 %collective-permute-start.1 = (bf16[2,128,512]{2,1,0:T(8,128)(2,1)S(1)}, bf16[2,128,512]{2,1,0:T(8,128)(2,1)S(1)}, u32[]{:S(2)}, u32[]{:S(2)}) collective-permute-start(bf16[2,128,512]{2,1,0:T(8,128)(2,1)S(1)} %pad_maximum_fusion.4), channel_id=1, source_target_pairs={{0,2},{1,3},{2,0},{3,1},{4,6},{5,7},{6,4},{7,5},{8,10},{9,11},{10,... | collective-permute-start | bytes 786440 | tf_op jit(solution)/shard_map/ppermute | solution.py:21
  14.3 5.9 %collective-permute-done.1 = bf16[2,128,512]{2,1,0:T(8,128)(2,1)S(1)} collective-permute-done((bf16[2,128,512]{2,1,0:T(8,128)(2,1)S(1)}, bf16[2,128,512]{2,1,0:T(8,128)(2,1)S(1)}, u32[]{:S(2)}, u32[]{:S(2)}) %collective-permute-start.1) | collective-permute-done | bytes 262176 | tf_op jit(solution)/shard_map/ppermute | solution.py:21
  20.3 1.8 collective-permute-start.2
  22.3 1.6 broadcast_in_dim.124
  24.2 15.2 %all_gather.37 = bf16[512,512]{1,0:T(8,128)(2,1)S(1)} all-gather(bf16[128,512]{1,0:T(8,128)(2,1)S(1)} %get-tuple-element.477), channel_id=1, replica_groups=mesh['row'=4,'col'=8] {'row'}, dimensions={0}, use_global_device_ids=true | all-gather | bytes 655360 | tf_op jit(solution)/shard_map/all_gather | solution.py:126
  42.1 7.4 %select_reduce_fusion.1 = (f32[8,512]{1,0:T(8,128)S(1)}, f32[8,512,1024]{2,1,0:T(8,128)}) fusion(pred[512,1024]{1,0:T(8,128)(4,1)S(1)} %bitcast.186, bf16[512,8,64]{0,2,1:T(8,128)(2,1)S(1)} %bitcast.193, bf16[1024,8,64]{0,2,1:T(8,128)(2,1)S(1)} %reshape_reshape.6), kind=kOutput, calls=%fused_computation.25 | convolution fusion | flops 549449728 | bytes 18890752 | tf_op jit(solution)/shard_map/while/body/eval_jaxpr/qhd,khd->hqk/dot_general | solution.py:85
  49.4 1.5 copy.29
  51.0 7.6 %fusion.20 = bf16[8,64,512]{2,1,0:T(8,128)(2,1)S(1)} fusion(bf16[1024,8,64]{0,2,1:T(8,128)(2,1)S(1)} %bitcast.195, f32[8,512,1024]{2,1,0:T(8,128)} %get-tuple-element.488, f32[8,512]{1,0:T(8,128)S(1)} %get-tuple-element.487, pred[512,1024]{1,0:T(8,128)(4,1)S(1)} %bitcast.187), kind=kOutput, calls=%fused_computation.41 | convolution fusion | flops 553910272 | bytes 18890752 | tf_op jit(solution)/shard_map/while/body/eval_jaxpr/hqk,khd->qhd/dot_general | solution.py:92
  59.7 8.2 %fusion.6 = bf16[8,512]{1,0:T(8,128)(2,1)S(1)} fusion(f32[8,512,1024]{2,1,0:T(8,128)} %get-tuple-element.488, f32[8,512]{1,0:T(8,128)S(1)} %get-tuple-element.487, pred[512,1024]{1,0:T(8,128)(4,1)S(1)} %bitcast.188), kind=kLoop, calls=%fused_computation.26 | loop fusion | flops 16773120 | bytes 17326080 | tf_op jit(solution)/shard_map/while/body/eval_jaxpr/reduce_sum | solution.py:91
  67.9 14.0 %all-gather.1 = bf16[2048,8]{0,1:T(8,128)(2,1)S(1)} all-gather(bf16[512,8]{0,1:T(8,128)(2,1)S(1)} %bitcast.205), channel_id=3, replica_groups=mesh['row'=4,'col'=8] {'row'}, dimensions={0}, use_global_device_ids=true | all-gather | bytes 40960 | tf_op jit(solution)/shard_map/all_gather | solution.py:36
  81.9 14.2 %all-gather = bf16[2048,8]{0,1:T(8,128)(2,1)S(1)} all-gather(bf16[512,8]{0,1:T(8,128)(2,1)S(1)} %convert_bitcast_fusion.3), channel_id=2, replica_groups=mesh['row'=4,'col'=8] {'row'}, dimensions={0}, use_global_device_ids=true | all-gather | bytes 40960 | tf_op jit(solution)/shard_map/all_gather | solution.py:36
  96.1 11.0 %all-gather.11.cloned.1.call-done = bf16[4,512,512]{2,1,0:T(8,128)(2,1)} async-done(((bf16[1,512,512]{2,1,0:T(8,128)(2,1)}), bf16[4,512,512]{2,1,0:T(8,128)(2,1)}) %all-gather.11.cloned.1.call-update) | async-done | bytes 2097168 | tf_op jit(solution)/shard_map/all_gather | solution.py:36
  108.7 5.7 %while.24 = (s32[]{:T(128)}, f32[512,512]{0,1:T(8,128)S(1)}, f32[512,8]{0,1:T(8,128)S(1)}, f32[512,8]{0,1:T(8,128)S(1)}, bf16[4,512,8]{1,2,0:T(8,128)(2,1)S(1)},...) while((s32[]{:T(128)}, f32[512,512]{0,1:T(8,128)S(1)}, ...), condition=%wide.region_3.4_spmd, body=%wide.region_2.3_spmd.sunk | while | flops 1081349 | bytes 4866199 | solution.py:44
  114.5 1.4 fusion.115
  116.0 2.2 fusion.116
  118.5 1.8 convolution_convert_fusion
  121.0 1.3 collective-permute-done.3
  122.4 1.5 collective-permute-start.4
  124.0 6.8 %collective-permute-done.4 = bf16[2,128,512]{2,1,0:T(8,128)(2,1)S(1)} collective-permute-done((bf16[2,128,512]{2,1,0:T(8,128)(2,1)S(1)}, bf16[2,128,512]{2,1,0:T(8,128)(2,1)S(1)}, u32[]{:S(2)}, u32[]{:S(2)}) %collective-permute-start.4) | collective-permute-done | bytes 262176 | tf_op jit(solution)/shard_map/ppermute | solution.py:21
  131.0 1.5 collective-permute-start.5
  132.5 16.2 %all_gather.42 = bf16[512,512]{1,0:T(8,128)(2,1)S(1)} all-gather(bf16[128,512]{1,0:T(8,128)(2,1)S(1)} %get-tuple-element.474), channel_id=1, replica_groups=mesh['row'=4,'col'=8] {'row'}, dimensions={0}, use_global_device_ids=true | all-gather | bytes 655360 | tf_op jit(solution)/shard_map/all_gather | solution.py:126
  151.4 7.4 %select_reduce_fusion = (f32[8,512]{1,0:T(8,128)S(1)}, f32[8,512,1024]{2,1,0:T(8,128)}) fusion(pred[512,1024]{1,0:T(8,128)(4,1)S(1)} %bitcast.189, bf16[512,8,64]{0,2,1:T(8,128)(2,1)S(1)} %bitcast.192, bf16[1024,8,64]{0,2,1:T(8,128)(2,1)S(1)} %reshape_reshape.7), kind=kOutput, calls=%fused_computation.23 | convolution fusion | flops 549449728 | bytes 18890752 | tf_op jit(solution)/shard_map/while/body/eval_jaxpr/qhd,khd->hqk/dot_general | solution.py:85
  158.7 1.5 copy.37
  160.2 7.6 %fusion.23 = bf16[8,64,512]{2,1,0:T(8,128)(2,1)S(1)} fusion(bf16[1024,8,64]{0,2,1:T(8,128)(2,1)S(1)} %bitcast.196, f32[8,512,1024]{2,1,0:T(8,128)} %get-tuple-element.494, f32[8,512]{1,0:T(8,128)S(1)} %get-tuple-element.493, pred[512,1024]{1,0:T(8,128)(4,1)S(1)} %bitcast.190), kind=kOutput, calls=%fused_computation.42 | convolution fusion | flops 553910272 | bytes 18890752 | tf_op jit(solution)/shard_map/while/body/eval_jaxpr/hqk,khd->qhd/dot_general | solution.py:92
  168.9 8.5 %fusion.8 = bf16[8,512]{1,0:T(8,128)(2,1)S(1)} fusion(f32[8,512,1024]{2,1,0:T(8,128)} %get-tuple-element.494, f32[8,512]{1,0:T(8,128)S(1)} %get-tuple-element.493, pred[512,1024]{1,0:T(8,128)(4,1)S(1)} %bitcast.191), kind=kLoop, calls=%fused_computation.28 | loop fusion | flops 16773120 | bytes 17326080 | tf_op jit(solution)/shard_map/while/body/eval_jaxpr/reduce_sum | solution.py:91
  177.3 13.8 %all-gather.3 = bf16[2048,8]{0,1:T(8,128)(2,1)S(1)} all-gather(bf16[512,8]{0,1:T(8,128)(2,1)S(1)} %bitcast.204), channel_id=5, replica_groups=mesh['row'=4,'col'=8] {'row'}, dimensions={0}, use_global_device_ids=true | all-gather | bytes 40960 | tf_op jit(solution)/shard_map/all_gather | solution.py:36
  191.2 13.9 %all-gather.2 = bf16[2048,8]{0,1:T(8,128)(2,1)S(1)} all-gather(bf16[512,8]{0,1:T(8,128)(2,1)S(1)} %convert_bitcast_fusion.1), channel_id=4, replica_groups=mesh['row'=4,'col'=8] {'row'}, dimensions={0}, use_global_device_ids=true | all-gather | bytes 40960 | tf_op jit(solution)/shard_map/all_gather | solution.py:36
  205.1 8.6 %all-gather.15.cloned.1.call-done = bf16[4,512,512]{2,1,0:T(8,128)(2,1)} async-done(((bf16[1,512,512]{2,1,0:T(8,128)(2,1)}), bf16[4,512,512]{2,1,0:T(8,128)(2,1)}) %all-gather.15.cloned.1.call-update) | async-done | bytes 2097168 | tf_op jit(solution)/shard_map/all_gather | solution.py:36
  215.2 5.7 %while.25 = (s32[]{:T(128)}, f32[512,512]{0,1:T(8,128)S(1)}, f32[512,8]{0,1:T(8,128)S(1)}, f32[512,8]{0,1:T(8,128)S(1)}, bf16[4,512,8]{1,2,0:T(8,128)(2,1)S(1)},...) while((s32[]{:T(128)}, f32[512,512]{0,1:T(8,128)S(1)}, ...), condition=%wide.region_11.12_spmd, body=%wide.region_10.11_spmd.sunk | while | flops 1081349 | bytes 4866199 | solution.py:44
  221.0 1.4 fusion.119
  222.6 2.2 fusion.120
  (114 shorter events, 27.7 us)
Async XLA Ops:
  6.5 3.2 %copy-start = (s32[32,32]{1,0:T(8,128)S(1)}, s32[32,32]{1,0:T(8,128)}, u32[]{:S(2)}) copy-start(s32[32,32]{1,0:T(8,128)} %param.13) | copy-start | bytes 12292
  6.5 42.9 %all-gather.9.cloned.1.call-start = ((), (), s32[]{:S(2)}) async-start(), calls=%async_computation | async-start | bytes 1179648 | tf_op jit(solution)/shard_map/all_gather | solution.py:124
  9.1 1.5 collective-permute-start
  9.6 97.5 %all-gather.11.cloned.1.call-start = ((), (), s32[]{:S(2)}) async-start(), calls=%async_computation.1 | async-start | bytes 2621440 | tf_op jit(solution)/shard_map/all_gather | solution.py:36
  10.6 9.5 %collective-permute-start.1 = (bf16[2,128,512]{2,1,0:T(8,128)(2,1)S(1)}, bf16[2,128,512]{2,1,0:T(8,128)(2,1)S(1)}, u32[]{:S(2)}, u32[]{:S(2)}) collective-permute-start(bf16[2,128,512]{2,1,0:T(8,128)(2,1)S(1)} %pad_maximum_fusion.4), channel_id=1, source_target_pairs={{0,2},{1,3},{2,0},{3,1},{4,6},{5,7},{6,4},{7,5},{8,10},{9,11},{10,... | collective-permute-start | bytes 786440 | tf_op jit(solution)/shard_map/ppermute | solution.py:21
  20.3 19.3 %collective-permute-start.2 = (bf16[4,128,512]{2,1,0:T(8,128)(2,1)S(1)}, bf16[4,128,512]{2,1,0:T(8,128)(2,1)}, u32[]{:S(2)}, u32[]{:S(2)}) collective-permute-start(bf16[4,128,512]{2,1,0:T(8,128)(2,1)S(1)} %pad_maximum_fusion.2), channel_id=1, source_target_pairs={{0,4},{1,5},{2,6},{3,7},{4,0},{5,1},{6,2},{7,3},{8,12},{9,13},{10,... | collective-permute-start | bytes 1572872 | tf_op jit(solution)/shard_map/ppermute | solution.py:21
  49.4 10.2 %copy-start.3 = (f32[2,2,512]{2,1,0:T(2,128)S(1)}, f32[2,2,512]{2,1,0:T(2,128)}, u32[]{:S(2)}) copy-start(f32[2,2,512]{2,1,0:T(2,128)} %param.18) | copy-start | bytes 24580
  49.4 10.2 %copy-start.4 = (f32[2,2,512]{2,1,0:T(2,128)S(1)}, f32[2,2,512]{2,1,0:T(2,128)}, u32[]{:S(2)}) copy-start(f32[2,2,512]{2,1,0:T(2,128)} %param.19) | copy-start | bytes 24580
  59.6 99.1 %all-gather.13.cloned.1.call-start = ((), (), s32[]{:S(2)}) async-start(), calls=%async_computation.2 | async-start | bytes 1179648 | tf_op jit(solution)/shard_map/all_gather | solution.py:124
  67.9 46.6 %copy-start.2 = (bf16[128,512]{1,0:T(8,128)(2,1)S(1)}, bf16[128,512]{1,0:T(8,128)(2,1)}, u32[]{:S(2)}) copy-start(bf16[128,512]{1,0:T(8,128)(2,1)} %param.12) | copy-start | bytes 393220
  121.0 1.3 collective-permute-start.3
  122.4 8.4 %collective-permute-start.4 = (bf16[2,128,512]{2,1,0:T(8,128)(2,1)S(1)}, bf16[2,128,512]{2,1,0:T(8,128)(2,1)S(1)}, u32[]{:S(2)}, u32[]{:S(2)}) collective-permute-start(bf16[2,128,512]{2,1,0:T(8,128)(2,1)S(1)} %pad_maximum_fusion.5), channel_id=1, source_target_pairs={{0,2},{1,3},{2,0},{3,1},{4,6},{5,7},{6,4},{7,5},{8,10},{9,11},{10,... | collective-permute-start | bytes 786440 | tf_op jit(solution)/shard_map/ppermute | solution.py:21
  124.0 89.7 %all-gather.15.cloned.1.call-start = ((), (), s32[]{:S(2)}) async-start(), calls=%async_computation.3 | async-start | bytes 2621440 | tf_op jit(solution)/shard_map/all_gather | solution.py:36
  131.0 17.9 %collective-permute-start.5 = (bf16[4,128,512]{2,1,0:T(8,128)(2,1)S(1)}, bf16[4,128,512]{2,1,0:T(8,128)(2,1)}, u32[]{:S(2)}, u32[]{:S(2)}) collective-permute-start(bf16[4,128,512]{2,1,0:T(8,128)(2,1)S(1)} %pad_maximum_fusion.3), channel_id=1, source_target_pairs={{0,4},{1,5},{2,6},{3,7},{4,0},{5,1},{6,2},{7,3},{8,12},{9,13},{10,... | collective-permute-start | bytes 1572872 | tf_op jit(solution)/shard_map/ppermute | solution.py:21
  213.7 12.1 %copy-start.1 = (s32[32,32]{1,0:T(8,128)S(1)}, s32[32,32]{1,0:T(8,128)}, u32[]{:S(2)}) copy-start(s32[32,32]{1,0:T(8,128)} %param.13) | copy-start | bytes 12292
Sparse Core Ops, SparseCore 0:
  9.7 29.1 all-gather.8
  59.7 47.3 all-gather.10
  124.1 24.6 all-gather.12
  169.0 44.6 all-gather.14
